TPU v7x, 32 devices: a whole 2x2x4 slice. The times are simulated.
32 devices in a mesh: plane: 8 (over z, x), wall: 4 (over y, core).
Axes of the slice: x: 2, y: 2, z: 4, core: 2. Of those that a mesh axis runs over, the one named last changes fastest.
Arguments:
- state: float32 [5, 125, 4, 1024], P(None, None, 'wall', 'plane'), may hold values from -6 to 6
- rhs: float32 [5, 125, 4, 1024], P(None, None, 'wall', 'plane'), may hold values from -6 to 6
- pivot_inv: float32 [125, 125, 4, 1024], P(None, None, 'wall', 'plane'), may hold values from -0.08944272 to 1.3394427
- coupling: float32 [125, 125, 4, 1024], P(None, None, 'wall', 'plane'), may hold values from -1.3 to 0.1
- face_coupling: float32 [4, 25, 25, 4, 1024], P(None, None, None, 'wall', 'plane'), may hold values from -1.25 to 1.25
- neighbors: int32 [1024, 4], P('plane'), may hold values from 0 to 1023, as said below
- counts: int32 [1024], P('plane'), may hold values from 2 to 4
Outputs:
- new_state: float32 [5, 125, 4, 1024], P(None, None, 'wall', 'plane')
- mean_square: float32 [], replicated
Inputs may be any that keep to these rules, and one draw needn't show every extreme that they name: neighbors[l, f] is the line across face f of line l (0 next streamwise, 1 previous streamwise, 2 next spanwise, 3 previous spanwise); the relation is mutual with faces 0 and 1, and 2 and 3, paired. Line l lies on index l // 128 of plane; its neighbours across faces 2 and 3 lie on the same index, those across faces 0 and 1 on the same index or the next or previous one, wrapping around.
All inputs are finite; a program needn't handle non-finite values.
Results may differ from a plain program's by a relative error of at most 0.0001.
Values sent between devices are 32-bit elements; how exact they have to be, the bound alone decides.
A program may use at most 128 MiB of HBM per device.

v0:
```python
import jax
import jax.numpy as jnp
from jax import lax
from jax.sharding import PartitionSpec as P

POINTS = 5
VARS = 5
DOFS = 125


highest = lax.Precision.HIGHEST
opposite = (1, 0, 3, 2)
relax_weight = 0.8


def with_halo(shard, sides, width):
    for axis, dim in sides:
        peers, length = (lax.axis_size(axis), shard.shape[dim])
        up = [(i, (i + 1) % peers) for i in range(peers)]
        down = [(j, i) for i, j in up]
        last = lax.slice_in_dim(shard, length - width, length, axis=dim)
        initial = lax.slice_in_dim(shard, 0, width, axis=dim)
        before = lax.ppermute(last, axis, up)
        after = lax.ppermute(initial, axis, down)
        shard = jnp.concatenate([before, shard, after], axis=dim)
    return shard


def from_behind(value, axis, steps):
    count = lax.axis_size(axis)
    initial, last = (max(0, -steps), min(count, count - steps))
    return lax.ppermute(value, axis, [(source, source + steps) for source in range(initial, last)])


def face_traces(state):
    tail = state.shape[2:]
    top_index = POINTS - 1
    cube = state.reshape((VARS, POINTS, POINTS, POINTS) + tail)
    faces = (cube[:, top_index], cube[:, 0], cube[:, :, :, top_index], cube[:, :, :, 0])
    return tuple((face.reshape((VARS, POINTS * POINTS) + tail) for face in faces))


def lift_faces(fluxes, tail):
    top_index = POINTS - 1
    cube = jnp.zeros((VARS, POINTS, POINTS, POINTS) + tail, jnp.float32)
    shaped = [flux.reshape((VARS, POINTS, POINTS) + tail) for flux in fluxes]
    cube = cube.at[:, top_index].add(shaped[0])
    cube = cube.at[:, 0].add(shaped[1])
    cube = cube.at[:, :, :, top_index].add(shaped[2])
    cube = cube.at[:, :, :, 0].add(shaped[3])
    return cube.reshape((VARS, POINTS * POINTS * POINTS) + tail)


def apply_block(block, vector):
    return jnp.einsum("jkl,vkl->vjl", block, vector, precision=highest)


def apply_transposed(block, vector):
    return jnp.einsum("kjl,vkl->vjl", block, vector, precision=highest)


def forward_sweep(residual, pivot_inv, coupling, active, incoming):
    carried = incoming
    inner = residual[:, :, 0] - apply_block(coupling[:, :, 0], carried)
    carried = active[0] * apply_block(pivot_inv[:, :, 0], inner)
    values = [carried]
    return (jnp.stack(values, axis=2), carried)


def backward_sweep(forward, pivot_inv, coupling, active, incoming):
    above = incoming
    values = [None] * forward.shape[2]
    for position in reversed(range(forward.shape[2])):
        value = active[position] * (
            forward[:, :, position] - apply_block(pivot_inv[:, :, position], above)
        )
        values[position] = value
        above = apply_transposed(coupling[:, :, position], value)
    return (jnp.stack(values, axis=2), above)


def body(state, rhs, pivot_inv, coupling, face_coupling, neighbors, counts):
    tail = state.shape[2:]
    elem_local = state.shape[2]
    line_local = state.shape[3]
    plane_size = lax.axis_size("plane")
    wall_size = lax.axis_size("wall")
    plane_index = lax.axis_index("plane")
    traces = face_traces(state)
    owner = neighbors // line_local
    slot_index = neighbors % line_local
    block_of = (owner - plane_index + 1) % plane_size
    extended = with_halo(jnp.stack(traces), (("plane", 4),), line_local)
    location = block_of * line_local + slot_index
    received = [jnp.take(extended[opposite[face]], location[:, face], axis=3) for face in range(4)]
    fluxes = [
        jnp.einsum("mnel,vnel->vmel", face_coupling[face], received[face], precision=highest)
        for face in range(4)
    ]
    residual = rhs - lift_faces(fluxes, tail)
    total = lax.psum(jnp.sum(residual * residual), ("plane", "wall"))
    mean_square = total / float(residual.size * plane_size * wall_size)
    wall_position = lax.axis_index("wall") * elem_local + jnp.arange(elem_local, dtype=jnp.int32)
    active = (wall_position[:, None] < counts[None, :]).astype(jnp.float32)
    zero_vector = jnp.zeros((VARS, DOFS, line_local), jnp.float32)

    def forward_relay(turn_index, incoming):
        outgoing = forward_sweep(residual, pivot_inv, coupling, active, incoming)[1]
        return from_behind(outgoing, "wall", 1)

    below = lax.fori_loop(0, wall_size - 1, forward_relay, zero_vector)
    forward, _ = forward_sweep(residual, pivot_inv, coupling, active, below)

    def backward_relay(turn_index, incoming):
        outgoing = backward_sweep(forward, pivot_inv, coupling, active, incoming)[1]
        return from_behind(outgoing, "wall", -1)

    above = lax.fori_loop(0, wall_size - 1, backward_relay, zero_vector)
    solution, _ = backward_sweep(forward, pivot_inv, coupling, active, above)
    new_state = (1.0 - relax_weight) * state + relax_weight * solution
    return (new_state, mean_square)


def solution(mesh):
    placed = (
        P(None, None, "wall", "plane"),
        P(None, None, "wall", "plane"),
        P(None, None, "wall", "plane"),
        P(None, None, "wall", "plane"),
        P(None, None, None, "wall", "plane"),
        P("plane", None),
        P("plane"),
    )
    return jax.shard_map(
        body,
        mesh=mesh,
        in_specs=placed,
        out_specs=(P(None, None, "wall", "plane"), P()),
        check_vma=False,
    )
```

profile of v0, /device:TPU:0, one launch (start us, length us, event | category | flops | bytes accessed | tf_op | source)
XLA Modules:
  0.0 399.5 jit_solution(13820128968304816088)
XLA Ops:
  0.7 1.0 fusion.118
  1.6 0.9 fusion.119
  2.8 3.0 collective-permute-start.2
  5.8 3.1 collective-permute-start.3
  8.9 0.7 fusion.110
  9.6 0.6 compare_and_fusion
  10.2 1.4 fusion.116
  11.7 1.1 copy.78
  12.7 2.3 copy.119
  15.0 2.3 copy.121
  17.3 2.4 copy.123
  19.7 1.6 copy.125
  21.6 13.3 %copy.105 = f32[125,125,1,128]{1,0,3,2:T(8,128)} copy(f32[125,125,1,128]{3,2,1,0:T(1,128)} %param.23) | data formatting | bytes 16000000 | tf_op jit(solution)/shard_map/while | solution.py:111
  34.9 13.3 %copy.104 = f32[125,125,1,128]{1,0,3,2:T(8,128)} copy(f32[125,125,1,128]{3,2,1,0:T(1,128)} %param.24) | data formatting | bytes 16000000 | tf_op jit(solution)/shard_map/while | solution.py:111
  48.2 0.5 compare_convert_fusion
  48.7 1.4 pad_maximum_fusion
  50.2 1.1 fusion.117
  51.3 1.7 copy.118
  53.0 2.9 gather_fusion
  55.9 5.2 %fusion.52 = f32[5,25,1,128]{1,0,3,2:T(8,128)S(1)} fusion(f32[1,25,25,1,128]{2,1,4,3,0:T(8,128)} %copy.119, f32[128,5,25]{2,1,0:T(8,128)} %gather_fusion, pred[128]{0:T(512)(128)(4,1)} %get-tuple-element.223), kind=kOutput, calls=%fused_computation.36 | convolution fusion | flops 4816000 | bytes 448128 | tf_op jit(solution)/shard_map/mnel,vnel->vmel/dot_general | solution.py:97
  61.1 0.8 copy.89
  61.9 2.6 copy.120
  64.5 2.9 gather_fusion.1
  67.4 5.2 %fusion.55 = f32[5,25,1,128]{1,0,3,2:T(8,128)S(1)} fusion(f32[1,25,25,1,128]{2,1,4,3,0:T(8,128)} %copy.121, f32[128,5,25]{2,1,0:T(8,128)} %gather_fusion.1, pred[128]{0:T(512)(128)(4,1)S(1)} %copy-done.9), kind=kOutput, calls=%fused_computation.37 | convolution fusion | flops 4816000 | bytes 448128 | tf_op jit(solution)/shard_map/mnel,vnel->vmel/dot_general | solution.py:97
  72.5 0.8 copy.92
  73.3 1.7 copy.122
  75.0 2.8 gather_fusion.2
  77.8 5.2 %fusion.58 = f32[5,25,1,128]{1,0,3,2:T(8,128)S(1)} fusion(f32[1,25,25,1,128]{2,1,4,3,0:T(8,128)} %copy.123, f32[128,5,25]{2,1,0:T(8,128)} %gather_fusion.2, pred[128]{0:T(512)(128)(4,1)S(1)} %copy-done.8), kind=kOutput, calls=%fused_computation.38 | convolution fusion | flops 4816000 | bytes 448128 | tf_op jit(solution)/shard_map/mnel,vnel->vmel/dot_general | solution.py:97
  83.2 2.1 copy.124
  85.3 2.9 gather_fusion.3
  88.2 4.5 %fusion.61 = f32[5,25,1,128]{1,0,3,2:T(8,128)S(1)} fusion(f32[1,25,25,1,128]{2,1,4,3,0:T(8,128)S(1)} %copy.125, f32[128,5,25]{2,1,0:T(8,128)} %gather_fusion.3, pred[128]{0:T(512)(128)(4,1)S(1)} %get-tuple-element.199), kind=kOutput, calls=%fused_computation.39 | convolution fusion | flops 4816000 | bytes 448128 | tf_op jit(solution)/shard_map/mnel,vnel->vmel/dot_general | solution.py:97
  92.9 3.3 scatter-add.15
  96.9 0.8 multiply_reduce_fusion
  97.7 109.9 %while.24 = (s32[]{:T(128)}, f32[5,125,128]{1,0,2:T(8,128)S(1)}, f32[1,128]{1,0:T(1,128)S(1)}, f32[5,125,1,128]{1,0,3,2:T(8,128)S(1)}, f32[125,125,1,128]{1,0,3,...) while((s32[]{:T(128)}, f32[5,125,128]{1,0,2:T(8,128)S(1)}, f32[1,128]{1,0:T(1,128)S(1)}, ...), condition=%wide.region_1.3_spmd, body=%wide.region_0.2_spmd.sunk | while | flops 240160000 | bytes 50880656 | solution.py:111
  97.7 15.5 %fusion.144 = f32[5,125,128]{1,0,2:T(8,128)S(1)} fusion(f32[5,125,128]{1,0,2:T(8,128)S(1)} %get-tuple-element.311, f32[125,125,1,128]{1,0,3,2:T(8,128)} %get-tuple-element.321, f32[5,125,1,128]{1,0,3,2:T(8,128)S(1)} %get-tuple-element.320), kind=kOutput, calls=%fused_computation.11.clone.1 | convolution fusion | flops 120080000 | bytes 8960000 | tf_op jit(solution)/shard_map/while/body/eval_jaxpr/jkl,vkl->vjl/dot_general | solution.py:55
  113.2 13.1 %fusion.145 = f32[5,125,128]{1,0,2:T(8,128)S(1)} fusion(f32[5,125,128]{1,0,2:T(8,128)S(1)} %fusion.144, f32[125,125,1,128]{1,0,3,2:T(8,128)S(1)} %copy-done, f32[128]{0:T(128)S(1)} %bitcast.282), kind=kOutput, calls=%fused_computation.9.clone.1 | convolution fusion | flops 120080000 | bytes 8640512 | tf_op jit(solution)/shard_map/while/body/eval_jaxpr/jkl,vkl->vjl/dot_general | solution.py:55
  126.4 1.5 collective-permute-start
  127.9 1.5 collective-permute-done
  129.4 15.5 %fusion.144 = f32[5,125,128]{1,0,2:T(8,128)S(1)} fusion(f32[5,125,128]{1,0,2:T(8,128)S(1)} %get-tuple-element.311, f32[125,125,1,128]{1,0,3,2:T(8,128)} %get-tuple-element.321, f32[5,125,1,128]{1,0,3,2:T(8,128)S(1)} %get-tuple-element.320), kind=kOutput, calls=%fused_computation.11.clone.1 | convolution fusion | flops 120080000 | bytes 8960000 | tf_op jit(solution)/shard_map/while/body/eval_jaxpr/jkl,vkl->vjl/dot_general | solution.py:55
  144.9 13.1 %fusion.145 = f32[5,125,128]{1,0,2:T(8,128)S(1)} fusion(f32[5,125,128]{1,0,2:T(8,128)S(1)} %fusion.144, f32[125,125,1,128]{1,0,3,2:T(8,128)S(1)} %copy-done, f32[128]{0:T(128)S(1)} %bitcast.282), kind=kOutput, calls=%fused_computation.9.clone.1 | convolution fusion | flops 120080000 | bytes 8640512 | tf_op jit(solution)/shard_map/while/body/eval_jaxpr/jkl,vkl->vjl/dot_general | solution.py:55
  158.0 8.7 %collective-permute-start = (f32[5,125,128]{1,0,2:T(8,128)S(1)}, f32[5,125,128]{1,0,2:T(8,128)S(1)}, u32[]{:S(2)}, u32[]{:S(2)}) collective-permute-start(f32[5,125,128]{1,0,2:T(8,128)S(1)} %fusion.145), channel_id=1, source_target_pairs={{0,1},{1,2},{2,3},{4,5},{5,6},{6,7},{8,9},{9,10},{10,11},{12,13},{... | collective-permute-start | bytes 960008 | tf_op jit(solution)/shard_map/while/body/eval_jaxpr/ppermute | solution.py:32
  166.8 1.5 collective-permute-done
  168.3 15.5 %fusion.144 = f32[5,125,128]{1,0,2:T(8,128)S(1)} fusion(f32[5,125,128]{1,0,2:T(8,128)S(1)} %get-tuple-element.311, f32[125,125,1,128]{1,0,3,2:T(8,128)} %get-tuple-element.321, f32[5,125,1,128]{1,0,3,2:T(8,128)S(1)} %get-tuple-element.320), kind=kOutput, calls=%fused_computation.11.clone.1 | convolution fusion | flops 120080000 | bytes 8960000 | tf_op jit(solution)/shard_map/while/body/eval_jaxpr/jkl,vkl->vjl/dot_general | solution.py:55
  183.8 13.1 %fusion.145 = f32[5,125,128]{1,0,2:T(8,128)S(1)} fusion(f32[5,125,128]{1,0,2:T(8,128)S(1)} %fusion.144, f32[125,125,1,128]{1,0,3,2:T(8,128)S(1)} %copy-done, f32[128]{0:T(128)S(1)} %bitcast.282), kind=kOutput, calls=%fused_computation.9.clone.1 | convolution fusion | flops 120080000 | bytes 8640512 | tf_op jit(solution)/shard_map/while/body/eval_jaxpr/jkl,vkl->vjl/dot_general | solution.py:55
  196.9 9.0 %collective-permute-start = (f32[5,125,128]{1,0,2:T(8,128)S(1)}, f32[5,125,128]{1,0,2:T(8,128)S(1)}, u32[]{:S(2)}, u32[]{:S(2)}) collective-permute-start(f32[5,125,128]{1,0,2:T(8,128)S(1)} %fusion.145), channel_id=1, source_target_pairs={{0,1},{1,2},{2,3},{4,5},{5,6},{6,7},{8,9},{9,10},{10,11},{12,13},{... | collective-permute-start | bytes 960008 | tf_op jit(solution)/shard_map/while/body/eval_jaxpr/ppermute | solution.py:32
  206.0 1.5 collective-permute-done
  207.6 15.5 %fusion.67 = f32[5,125,128]{1,0,2:T(8,128)S(1)} fusion(f32[5,125,128]{1,0,2:T(8,128)S(1)} %get-tuple-element.115, f32[125,125,1,128]{1,0,3,2:T(8,128)} %get-tuple-element.347, f32[5,125,1,128]{1,0,3,2:T(8,128)S(1)} %get-tuple-element.348), kind=kOutput, calls=%fused_computation.41 | convolution fusion | flops 120080000 | bytes 8960000 | tf_op jit(solution)/shard_map/jkl,vkl->vjl/dot_general | solution.py:55
  223.2 13.1 %fusion.49 = f32[5,125,128]{1,0,2:T(8,128)S(1)} fusion(f32[5,125,128]{1,0,2:T(8,128)S(1)} %fusion.67, f32[125,125,1,128]{1,0,3,2:T(8,128)S(1)} %copy-done.1, f32[128]{0:T(128)S(1)} %copy-done.10), kind=kOutput, calls=%fused_computation.35 | convolution fusion | flops 120080000 | bytes 8640512 | tf_op jit(solution)/shard_map/jkl,vkl->vjl/dot_general | solution.py:55
  236.4 100.8 %while.25 = (s32[]{:T(128)}, f32[5,125,128]{1,0,2:T(8,128)S(1)}, f32[1,128]{1,0:T(1,128)S(1)}, f32[125,125,1,128]{1,0,3,2:T(8,128)}, f32[5,125,128]{1,0,2:T(8,128)S(1)}, /*index=5*/f32[125,125,1,128]{1,0,3,2:T(8,128)}, s32[]{:T(128)}) while((s32[]{:T(128)}, f32[5,125,128]{1,0,2:T(8,128)S(1)}, f32[1,128]{1,0:T(1,128)S(1)}, ...), condition=%wide.region_3.5_spmd, body=%wide.region_2.4_spmd.sunk | while | flops 240160000 | bytes 50880656 | solution.py:118
  236.6 15.5 %fusion.150 = f32[5,125,128]{1,0,2:T(8,128)S(1)} fusion(f32[5,125,128]{1,0,2:T(8,128)S(1)} %get-tuple-element.342, f32[5,125,128]{1,0,2:T(8,128)S(1)} %get-tuple-element.332, f32[125,125,1,128]{1,0,3,2:T(8,128)} %get-tuple-element.341, f32[128]{0:T(128)S(1)} %bitcast.283), kind=kOutput, calls=%fused_computation.18.clone.1 | convolution fusion | flops 120160000 | bytes 8960512 | tf_op jit(solution)/shard_map/while/body/eval_jaxpr/jkl,vkl->vjl/dot_general | solution.py:55
  252.1 7.3 %fusion.151 = f32[5,125,128]{1,0,2:T(8,128)S(1)} fusion(f32[5,125,128]{1,0,2:T(8,128)S(1)} %fusion.150, f32[125,125,1,128]{1,0,3,2:T(8,128)S(1)} %copy-done.2), kind=kOutput, calls=%fused_computation.19.clone.1 | convolution fusion | flops 120000000 | bytes 8640000 | tf_op jit(solution)/shard_map/while/body/eval_jaxpr/kjl,vkl->vjl/dot_general | solution.py:59
  259.4 1.3 collective-permute-start.1
  260.7 9.1 %collective-permute-done.1 = f32[5,125,128]{1,0,2:T(8,128)S(1)} collective-permute-done((f32[5,125,128]{1,0,2:T(8,128)S(1)}, f32[5,125,128]{1,0,2:T(8,128)S(1)}, u32[]{:S(2)}, u32[]{:S(2)}) %collective-permute-start.1) | collective-permute-done | bytes 320032 | tf_op jit(solution)/shard_map/while/body/eval_jaxpr/ppermute | solution.py:32
  269.8 15.5 %fusion.150 = f32[5,125,128]{1,0,2:T(8,128)S(1)} fusion(f32[5,125,128]{1,0,2:T(8,128)S(1)} %get-tuple-element.342, f32[5,125,128]{1,0,2:T(8,128)S(1)} %get-tuple-element.332, f32[125,125,1,128]{1,0,3,2:T(8,128)} %get-tuple-element.341, f32[128]{0:T(128)S(1)} %bitcast.283), kind=kOutput, calls=%fused_computation.18.clone.1 | convolution fusion | flops 120160000 | bytes 8960512 | tf_op jit(solution)/shard_map/while/body/eval_jaxpr/jkl,vkl->vjl/dot_general | solution.py:55
  285.3 7.3 %fusion.151 = f32[5,125,128]{1,0,2:T(8,128)S(1)} fusion(f32[5,125,128]{1,0,2:T(8,128)S(1)} %fusion.150, f32[125,125,1,128]{1,0,3,2:T(8,128)S(1)} %copy-done.2), kind=kOutput, calls=%fused_computation.19.clone.1 | convolution fusion | flops 120000000 | bytes 8640000 | tf_op jit(solution)/shard_map/while/body/eval_jaxpr/kjl,vkl->vjl/dot_general | solution.py:59
  292.6 1.3 collective-permute-start.1
  293.9 9.9 %collective-permute-done.1 = f32[5,125,128]{1,0,2:T(8,128)S(1)} collective-permute-done((f32[5,125,128]{1,0,2:T(8,128)S(1)}, f32[5,125,128]{1,0,2:T(8,128)S(1)}, u32[]{:S(2)}, u32[]{:S(2)}) %collective-permute-start.1) | collective-permute-done | bytes 320032 | tf_op jit(solution)/shard_map/while/body/eval_jaxpr/ppermute | solution.py:32
  303.9 15.5 %fusion.150 = f32[5,125,128]{1,0,2:T(8,128)S(1)} fusion(f32[5,125,128]{1,0,2:T(8,128)S(1)} %get-tuple-element.342, f32[5,125,128]{1,0,2:T(8,128)S(1)} %get-tuple-element.332, f32[125,125,1,128]{1,0,3,2:T(8,128)} %get-tuple-element.341, f32[128]{0:T(128)S(1)} %bitcast.283), kind=kOutput, calls=%fused_computation.18.clone.1 | convolution fusion | flops 120160000 | bytes 8960512 | tf_op jit(solution)/shard_map/while/body/eval_jaxpr/jkl,vkl->vjl/dot_general | solution.py:55
  319.4 7.3 %fusion.151 = f32[5,125,128]{1,0,2:T(8,128)S(1)} fusion(f32[5,125,128]{1,0,2:T(8,128)S(1)} %fusion.150, f32[125,125,1,128]{1,0,3,2:T(8,128)S(1)} %copy-done.2), kind=kOutput, calls=%fused_computation.19.clone.1 | convolution fusion | flops 120000000 | bytes 8640000 | tf_op jit(solution)/shard_map/while/body/eval_jaxpr/kjl,vkl->vjl/dot_general | solution.py:59
  326.7 1.3 collective-permute-start.1
  328.0 9.2 %collective-permute-done.1 = f32[5,125,128]{1,0,2:T(8,128)S(1)} collective-permute-done((f32[5,125,128]{1,0,2:T(8,128)S(1)}, f32[5,125,128]{1,0,2:T(8,128)S(1)}, u32[]{:S(2)}, u32[]{:S(2)}) %collective-permute-start.1) | collective-permute-done | bytes 320032 | tf_op jit(solution)/shard_map/while/body/eval_jaxpr/ppermute | solution.py:32
  337.2 15.6 %fusion.85 = f32[5,125,1,128]{1,0,3,2:T(8,128)S(1)} fusion(f32[5,125,128]{1,0,2:T(8,128)S(1)} %get-tuple-element.350, f32[5,125,128]{1,0,2:T(8,128)S(1)} %get-tuple-element.116, f32[125,125,1,128]{1,0,3,2:T(8,128)} %get-tuple-element.346, f32[5,125,1,128]{1,0,3,2:T(8,128)S(1)} %copy-done.3, f32[128]{0:T(128)S(1)} %copy-done.10), kind=kOutput, calls=%fused_computation.47 | convolution fusion | flops 120400000 | bytes 9280512 | tf_op jit(solution)/shard_map/jkl,vkl->vjl/dot_general | solution.py:55
  352.8 0.9 copy.111
  353.8 43.7 %psum.7 = f32[]{:T(128)} all-reduce(f32[]{:T(128)} %get-tuple-element.197), channel_id=1, replica_groups=mesh['plane'=8,'wall'=4] {'plane','wall'}, use_global_device_ids=true, to_apply=%region_5.7 | all-reduce | flops 1 | bytes 8 | tf_op jit(solution)/shard_map/psum | solution.py:101
  (48 shorter events, 1.7 us)
Async XLA Ops:
  0.6 11.0 %copy-start.4 = (f32[5,125,1,128]{3,2,1,0:T(1,128)S(1)}, f32[5,125,1,128]{3,2,1,0:T(1,128)}, u32[]{:S(2)}) copy-start(f32[5,125,1,128]{3,2,1,0:T(1,128)} %param.21) | copy-start | bytes 960004
  0.6 11.0 %copy-start.11 = (s32[128]{0:T(128)S(1)}, s32[128]{0:T(128)}, u32[]{:S(2)}) copy-start(s32[128]{0:T(128)} %param.27) | copy-start | bytes 1540
  2.8 46.0 %collective-permute-start.2 = (f32[4,5,25,1,128]{4,0,3,2,1:T(4,128)S(1)}, f32[4,5,25,1,128]{4,0,3,2,1:T(4,128)}, u32[]{:S(2)}, u32[]{:S(2)}) collective-permute-start(f32[4,5,25,1,128]{4,0,3,2,1:T(4,128)S(1)} %pad_maximum_fusion.1), channel_id=1, source_target_pairs={{0,4},{4,8},{8,12},{12,16},{16,20},{20,24},{24,28},{28,0},{1,5},{5... | collective-permute-start | bytes 768008 | tf_op jit(solution)/shard_map/ppermute | solution.py:23
  5.8 42.9 %collective-permute-start.3 = (f32[4,5,25,1,128]{4,0,3,2,1:T(4,128)S(1)}, f32[4,5,25,1,128]{4,0,3,2,1:T(4,128)}, u32[]{:S(2)}, u32[]{:S(2)}) collective-permute-start(f32[4,5,25,1,128]{4,0,3,2,1:T(4,128)S(1)} %pad_maximum_fusion.1), channel_id=1, source_target_pairs={{4,0},{8,4},{12,8},{16,12},{20,16},{24,20},{28,24},{0,28},{5,1},{9... | collective-permute-start | bytes 768008 | tf_op jit(solution)/shard_map/ppermute | solution.py:24
  17.3 4.0 %copy-start.5 = (f32[5,125,1,128]{3,2,1,0:T(1,128)S(1)}, f32[5,125,1,128]{3,2,1,0:T(1,128)}, u32[]{:S(2)}) copy-start(f32[5,125,1,128]{3,2,1,0:T(1,128)} %param.22) | copy-start | bytes 960004
  55.9 11.5 %copy-start.9 = (pred[128]{0:T(512)(128)(4,1)S(1)}, pred[128]{0:T(512)(128)(4,1)}, u32[]{:S(2)}) copy-start(pred[128]{0:T(512)(128)(4,1)} %get-tuple-element.221) | copy-start | bytes 388
  67.4 10.5 %copy-start.8 = (pred[128]{0:T(512)(128)(4,1)S(1)}, pred[128]{0:T(512)(128)(4,1)}, u32[]{:S(2)}) copy-start(pred[128]{0:T(512)(128)(4,1)} %get-tuple-element.219) | copy-start | bytes 388
  85.3 7.5 %copy-start.6 = (f32[5,25,1,128]{3,2,1,0:T(1,128)S(1)}, f32[5,25,1,128]{3,2,1,0:T(1,128)}, u32[]{:S(2)}) copy-start(f32[5,25,1,128]{3,2,1,0:T(1,128)} %copy.89) | copy-start | bytes 192004
  88.2 4.7 %copy-start.7 = (f32[5,25,1,128]{3,2,1,0:T(1,128)S(1)}, f32[5,25,1,128]{3,2,1,0:T(1,128)}, u32[]{:S(2)}) copy-start(f32[5,25,1,128]{3,2,1,0:T(1,128)} %copy.92) | copy-start | bytes 192004
  97.7 15.6 %copy-start = (f32[125,125,1,128]{1,0,3,2:T(8,128)S(1)}, f32[125,125,1,128]{1,0,3,2:T(8,128)}, u32[]{:S(2)}) copy-start(f32[125,125,1,128]{1,0,3,2:T(8,128)} %get-tuple-element.322) | copy-start | bytes 24000004 | tf_op jit(solution)/shard_map/while
  126.4 3.0 collective-permute-start
  129.4 15.5 %copy-start = (f32[125,125,1,128]{1,0,3,2:T(8,128)S(1)}, f32[125,125,1,128]{1,0,3,2:T(8,128)}, u32[]{:S(2)}) copy-start(f32[125,125,1,128]{1,0,3,2:T(8,128)} %get-tuple-element.322) | copy-start | bytes 24000004 | tf_op jit(solution)/shard_map/while
  158.0 10.2 %collective-permute-start = (f32[5,125,128]{1,0,2:T(8,128)S(1)}, f32[5,125,128]{1,0,2:T(8,128)S(1)}, u32[]{:S(2)}, u32[]{:S(2)}) collective-permute-start(f32[5,125,128]{1,0,2:T(8,128)S(1)} %fusion.145), channel_id=1, source_target_pairs={{0,1},{1,2},{2,3},{4,5},{5,6},{6,7},{8,9},{9,10},{10,11},{12,13},{... | collective-permute-start | bytes 960008 | tf_op jit(solution)/shard_map/while/body/eval_jaxpr/ppermute | solution.py:32
  168.3 15.5 %copy-start = (f32[125,125,1,128]{1,0,3,2:T(8,128)S(1)}, f32[125,125,1,128]{1,0,3,2:T(8,128)}, u32[]{:S(2)}) copy-start(f32[125,125,1,128]{1,0,3,2:T(8,128)} %get-tuple-element.322) | copy-start | bytes 24000004 | tf_op jit(solution)/shard_map/while
  196.9 10.5 %collective-permute-start = (f32[5,125,128]{1,0,2:T(8,128)S(1)}, f32[5,125,128]{1,0,2:T(8,128)S(1)}, u32[]{:S(2)}, u32[]{:S(2)}) collective-permute-start(f32[5,125,128]{1,0,2:T(8,128)S(1)} %fusion.145), channel_id=1, source_target_pairs={{0,1},{1,2},{2,3},{4,5},{5,6},{6,7},{8,9},{9,10},{10,11},{12,13},{... | collective-permute-start | bytes 960008 | tf_op jit(solution)/shard_map/while/body/eval_jaxpr/ppermute | solution.py:32
  207.6 15.6 %copy-start.1 = (f32[125,125,1,128]{1,0,3,2:T(8,128)S(1)}, f32[125,125,1,128]{1,0,3,2:T(8,128)}, u32[]{:S(2)}) copy-start(f32[125,125,1,128]{1,0,3,2:T(8,128)} %get-tuple-element.345) | copy-start | bytes 24000004
  207.6 15.6 %copy-start.10 = (f32[128]{0:T(128)S(1)}, f32[128]{0:T(128)}, u32[]{:S(2)}) copy-start(f32[128]{0:T(128)} %compare_convert_fusion) | copy-start | bytes 1540
  236.3 100.9 %copy-start.3 = (f32[5,125,1,128]{1,0,3,2:T(8,128)S(1)}, f32[5,125,1,128]{1,0,3,2:T(8,128)}, u32[]{:S(2)}) copy-start(f32[5,125,1,128]{1,0,3,2:T(8,128)} %copy.78) | copy-start | bytes 960004
  236.6 15.6 %copy-start.2 = (f32[125,125,1,128]{1,0,3,2:T(8,128)S(1)}, f32[125,125,1,128]{1,0,3,2:T(8,128)}, u32[]{:S(2)}) copy-start(f32[125,125,1,128]{1,0,3,2:T(8,128)} %get-tuple-element.343) | copy-start | bytes 24000004 | tf_op jit(solution)/shard_map/while
  259.4 10.4 %collective-permute-start.1 = (f32[5,125,128]{1,0,2:T(8,128)S(1)}, f32[5,125,128]{1,0,2:T(8,128)S(1)}, u32[]{:S(2)}, u32[]{:S(2)}) collective-permute-start(f32[5,125,128]{1,0,2:T(8,128)S(1)} %fusion.151), channel_id=1, source_target_pairs={{1,0},{2,1},{3,2},{5,4},{6,5},{7,6},{9,8},{10,9},{11,10},{13,12},{... | collective-permute-start | bytes 960008 | tf_op jit(solution)/shard_map/while/body/eval_jaxpr/ppermute | solution.py:32
  269.8 15.5 %copy-start.2 = (f32[125,125,1,128]{1,0,3,2:T(8,128)S(1)}, f32[125,125,1,128]{1,0,3,2:T(8,128)}, u32[]{:S(2)}) copy-start(f32[125,125,1,128]{1,0,3,2:T(8,128)} %get-tuple-element.343) | copy-start | bytes 24000004 | tf_op jit(solution)/shard_map/while
  292.6 11.2 %collective-permute-start.1 = (f32[5,125,128]{1,0,2:T(8,128)S(1)}, f32[5,125,128]{1,0,2:T(8,128)S(1)}, u32[]{:S(2)}, u32[]{:S(2)}) collective-permute-start(f32[5,125,128]{1,0,2:T(8,128)S(1)} %fusion.151), channel_id=1, source_target_pairs={{1,0},{2,1},{3,2},{5,4},{6,5},{7,6},{9,8},{10,9},{11,10},{13,12},{... | collective-permute-start | bytes 960008 | tf_op jit(solution)/shard_map/while/body/eval_jaxpr/ppermute | solution.py:32
  303.9 15.5 %copy-start.2 = (f32[125,125,1,128]{1,0,3,2:T(8,128)S(1)}, f32[125,125,1,128]{1,0,3,2:T(8,128)}, u32[]{:S(2)}) copy-start(f32[125,125,1,128]{1,0,3,2:T(8,128)} %get-tuple-element.343) | copy-start | bytes 24000004 | tf_op jit(solution)/shard_map/while
  326.7 10.5 %collective-permute-start.1 = (f32[5,125,128]{1,0,2:T(8,128)S(1)}, f32[5,125,128]{1,0,2:T(8,128)S(1)}, u32[]{:S(2)}, u32[]{:S(2)}) collective-permute-start(f32[5,125,128]{1,0,2:T(8,128)S(1)} %fusion.151), channel_id=1, source_target_pairs={{1,0},{2,1},{3,2},{5,4},{6,5},{7,6},{9,8},{10,9},{11,10},{13,12},{... | collective-permute-start | bytes 960008 | tf_op jit(solution)/shard_map/while/body/eval_jaxpr/ppermute | solution.py:32
where the time goes:
time: 404 us; the launch traced here: 399 us
  matrix products  219 us (54%)
  local copies, waits for them, and re-layouts  67.4 us (17%)
  blocking collectives  43.7 us (11%)
  waiting for transfers between devices  32.7 us (8%)
  starting transfers between devices  29.2 us (7%)
  other arithmetic  4.34 us (1%)
    dot_general x12, matrix products, apply_block(): return jnp.einsum('jkl,vkl->vjl', block, vector, precision=highest)  177 us
    psum x1, blocking collectives, body(): total = lax.psum(jnp.sum(residual * residual), ('plane', 'wall'))  43.7 us
    ppermute x6, waiting for transfers between devices, from_behind(): lax.ppermute(value, axis, [(source, source + steps) for source in range(i...  32.7 us
    while x2, local copies, waits for them, and re-layouts, body(): below = lax.fori_loop(0, wall_size - 1, forward_relay, zero_vector)  26.6 us
    ppermute x6, starting transfers between devices, from_behind(): lax.ppermute(value, axis, [(source, source + steps) for source in range(i...  23.1 us
    dot_general x3, matrix products, apply_transposed(): return jnp.einsum('kjl,vkl->vjl', block, vector, precision=highest)  21.9 us
    dot_general x4, matrix products, body(): jnp.einsum('mnel,vnel->vmel', face_coupling[face], received[face], precis...  20 us
    unnamed x31, local copies, waits for them, and re-layouts  18.9 us
  transfers between devices with their start and end apart: 8, of which 6 were waited for; matrix products, arithmetic and copies ran while one was open for 10% of the time, Pallas kernels for 0%

commit v1 on v0

v1 whole, which is shorter than its diff:
```python
import functools

import jax
import jax.numpy as jnp
from jax import lax
from jax.experimental import pallas as pl
from jax.experimental.pallas import tpu as pltpu
from jax.sharding import PartitionSpec as P

POINTS = 5
VARS = 5
DOFS = POINTS**3
FACE = POINTS**2
SUB = 8
TAIL = DOFS - SUB
GROUPS = -(-DOFS // SUB)
F32 = jnp.float32

STARTS = tuple(min(SUB * t, TAIL) for t in range(GROUPS))
FACE_STARTS = tuple(min(SUB * t, FACE - SUB) for t in range(-(-FACE // SUB)))
FACE_ROWS = ((DOFS - FACE, 1), (0, 1), (POINTS - 1, POINTS), (0, POINTS))


def sublanes():
    return lax.broadcasted_iota(jnp.int32, (SUB, 128), 0)


def row_sums(parts):
    sub = sublanes()

    def pair(x, y, shift):
        low = (sub & shift) == 0
        return jnp.where(low, x, y) + pltpu.roll(jnp.where(low, y, x), shift, 0)

    for shift in (1, 2, 4):
        parts = [pair(parts[i], parts[i + 1], shift) for i in range(0, len(parts), 2)]
    return parts[0]


def fresh_rows(tile, fresh):
    return jnp.where(sublanes() >= SUB - fresh, tile, 0.0)


def vector_tiles(load):
    tiles = [load(start) for start in STARTS]
    tiles[-1] = fresh_rows(tiles[-1], DOFS - SUB * (GROUPS - 1))
    return tiles


def apply_block(block, load, emit):
    tiles = vector_tiles(load)

    def group(g, carry):
        first = jnp.minimum(SUB * g, TAIL)
        parts = []
        for s in range(SUB):
            row = (first + s) * DOFS
            total = block[pl.ds(row, SUB), :] * tiles[0]
            for t in range(1, GROUPS):
                total = total + block[pl.ds(row + STARTS[t], SUB), :] * tiles[t]
            parts.append(total)
        emit(first, row_sums(parts))
        return carry

    lax.fori_loop(0, GROUPS, group, 0, unroll=2)


def apply_transposed(block, load_row, store):
    def step(j, totals):
        spread = jnp.broadcast_to(load_row(j), (SUB, 128))
        return tuple(
            totals[t] + block[pl.ds(j * DOFS + STARTS[t], SUB), :] * spread
            for t in range(GROUPS)
        )

    zeros = tuple(jnp.zeros((SUB, 128), F32) for _ in range(GROUPS))
    totals = lax.fori_loop(0, DOFS, step, zeros, unroll=5)
    for t in range(GROUPS):
        store(STARTS[t], totals[t])


def kernel(
    planes, walls, state, rhs, pivot, coupling, face, neighbors, counts, out, mean,
    st, r, pv, cp, fc, nb, ct, halo, fl, w, inner, below, x, back, above, fresh,
    ssq, plane_sums, wall_own, wall_sums,
    load_sem, out_sem, halo_send, halo_recv, fwd_send, fwd_recv, bwd_send, bwd_recv,
    plane_send, plane_recv, wall_send, wall_recv,
):
    me_p, me_w = lax.axis_index("plane"), lax.axis_index("wall")
    top = walls - 1

    loads = [
        pltpu.make_async_copy(state.at[:, :, 0, :], st.at[:, 0:DOFS, :], load_sem.at[0]),
        pltpu.make_async_copy(neighbors, nb, load_sem.at[1]),
        pltpu.make_async_copy(counts, ct, load_sem.at[2]),
        pltpu.make_async_copy(face.reshape(4 * FACE * FACE, 128), fc, load_sem.at[3]),
        pltpu.make_async_copy(rhs.at[:, :, 0, :], r.at[:, 0:DOFS, :], load_sem.at[4]),
    ]
    for load in loads:
        load.start()
    pivot_load = pltpu.make_async_copy(pivot.reshape(DOFS * DOFS, 128), pv, load_sem.at[5])
    coupling_load = pltpu.make_async_copy(
        coupling.reshape(DOFS * DOFS, 128), cp, load_sem.at[6]
    )

    barrier = pltpu.get_barrier_semaphore()
    for d in range(1, planes):
        pl.semaphore_signal(barrier, inc=1, device_id={"plane": lax.rem(me_p + d, planes)})
    for d in range(1, walls):
        pl.semaphore_signal(barrier, inc=1, device_id={"wall": lax.rem(me_w + d, walls)})

    pivot_load.start()

    @pl.when(me_w > 0)
    def _():
        coupling_load.start()

    pl.semaphore_wait(barrier, planes - 1 + walls - 1)

    def halo_copy(v, side, f):
        target = lax.rem(me_p + (1 if side == 0 else planes - 1), planes)
        return pltpu.make_async_remote_copy(
            src_ref=state.at[v, pl.ds(FACE_ROWS[f][0], FACE), 0, :],
            dst_ref=halo.at[v, side, f, 0:FACE, :],
            send_sem=halo_send.at[v, side, f],
            recv_sem=halo_recv.at[v, side, f],
            device_id={"plane": target},
        )

    def send_halo(v, carry):
        for side in range(2):
            for f in range(2):
                halo_copy(v, side, f).start()
        return carry

    lax.fori_loop(0, VARS, send_halo, 0)

    def fwd_copy(v):
        return pltpu.make_async_remote_copy(
            src_ref=w.at[v, 0:DOFS, :],
            dst_ref=below.at[v, 0:DOFS, :],
            send_sem=fwd_send.at[v],
            recv_sem=fwd_recv.at[v],
            device_id={"wall": lax.rem(me_w + 1, walls)},
        )

    def bwd_copy(v):
        return pltpu.make_async_remote_copy(
            src_ref=back.at[v, 0:DOFS, :],
            dst_ref=above.at[v, 0:DOFS, :],
            send_sem=bwd_send.at[v],
            recv_sem=bwd_recv.at[v],
            device_id={"wall": lax.rem(me_w + walls - 1, walls)},
        )

    def out_copy(v):
        return pltpu.make_async_copy(fresh.at[v, 0:DOFS, :], out.at[v, :, 0, :], out_sem.at[v])

    def plane_copy(d):
        return pltpu.make_async_remote_copy(
            src_ref=ssq,
            dst_ref=plane_sums.at[me_p],
            send_sem=plane_send.at[d],
            recv_sem=plane_recv.at[d],
            device_id={"plane": lax.rem(me_p + d, planes)},
        )

    def wall_copy(d):
        return pltpu.make_async_remote_copy(
            src_ref=wall_own,
            dst_ref=wall_sums.at[me_w],
            send_sem=wall_send.at[d],
            recv_sem=wall_recv.at[d],
            device_id={"wall": lax.rem(me_w + d, walls)},
        )

    ssq[...] = jnp.zeros((SUB, 128), F32)
    for load in loads:
        load.wait()
    active = jnp.broadcast_to(jnp.where(ct[...] > me_w, 1.0, 0.0).astype(F32), (SUB, 128))
    lane_bits = (st.shape[2] - 1).bit_length()

    def received_tiles(v, f):
        other = f ^ 1
        first, stride = FACE_ROWS[other]
        line = jnp.broadcast_to(nb[f : f + 1, :], (SUB, 128))
        slot = line & ((1 << lane_bits) - 1)
        away = (line >> lane_bits) - me_p
        here = away == 0
        before = (away == -1) | (away == planes - 1)

        def take(tile):
            return jnp.take_along_axis(tile, slot, axis=1, mode="promise_in_bounds")

        tiles = []
        for start in FACE_STARTS:
            if stride == 1:
                tile = take(st[v, pl.ds(first + start, SUB), :])
            else:
                tile = take(st[v, pl.ds(first + stride * start, SUB, stride=stride), :])
            if f < 2:
                low = take(halo[v, 0, other, pl.ds(start, SUB), :])
                high = take(halo[v, 1, other, pl.ds(start, SUB), :])
                tile = jnp.where(here, tile, jnp.where(before, low, high))
            tiles.append(tile)
        tiles[-1] = fresh_rows(tiles[-1], FACE - SUB * (len(FACE_STARTS) - 1))
        return tiles

    def residual(v):
        for f in (2, 3, 0, 1):
            if f == 0:
                for side in range(2):
                    for g in range(2):
                        halo_copy(v, side, g).wait_recv()
            tiles = received_tiles(v, f)

            def product(m):
                row = (f * FACE + m) * FACE
                total = fc[pl.ds(row, SUB), :] * tiles[0]
                for t in range(1, len(tiles)):
                    total = total + fc[pl.ds(row + FACE_STARTS[t], SUB), :] * tiles[t]
                return total

            whole = FACE // SUB * SUB
            for m in range(0, whole, SUB):
                fl[f, pl.ds(m, SUB), :] = row_sums([product(m + s) for s in range(SUB)])
            for m in range(whole, FACE):
                fl[f, pl.ds(m, 1), :] = jnp.sum(product(m), axis=0, keepdims=True)
        for f in range(4):
            first, stride = FACE_ROWS[f]
            rows = pl.ds(first, FACE) if stride == 1 else pl.ds(first, FACE, stride=stride)
            r[v, rows, :] = r[v, rows, :] - fl[f, 0:FACE, :]
        total = ssq[...]
        for tile in vector_tiles(lambda start: r[v, pl.ds(start, SUB), :]):
            total = total + tile * tile
        ssq[...] = total

    def forward(v, wall_element):
        if wall_element:
            source = lambda start: r[v, pl.ds(start, SUB), :]
        else:
            fwd_copy(v).wait_recv()

            def emit_inner(first, rows):
                inner[pl.ds(first, SUB), :] = r[v, pl.ds(first, SUB), :] - rows

            apply_block(cp, lambda start: below[v, pl.ds(start, SUB), :], emit_inner)
            source = lambda start: inner[pl.ds(start, SUB), :]

        def emit(first, rows):
            w[v, pl.ds(first, SUB), :] = active * rows

        apply_block(pv, source, emit)

        @pl.when(me_w < top)
        def _():
            fwd_copy(v).start()

    def send_down(v, source):
        def store(start, rows):
            back[v, pl.ds(start, SUB), :] = rows

        apply_transposed(cp, lambda j: source[v, pl.ds(j, 1), :], store)
        bwd_copy(v).start()

    def finish(v, source):
        for start in STARTS:
            rows = pl.ds(start, SUB)
            fresh[v, rows, :] = 0.2 * st[v, rows, :] + 0.8 * source[v, rows, :]
        out_copy(v).start()

    def first_loop(v, carry):
        residual(v)

        @pl.when(me_w == 0)
        def _():
            @pl.when(v == 0)
            def _():
                pivot_load.wait()

            forward(v, True)

        return carry

    lax.fori_loop(0, VARS, first_loop, 0)

    plane_sums[me_p] = ssq[...]
    for d in range(1, planes):
        plane_copy(d).start()

    @pl.when(me_w > 0)
    def _():
        pivot_load.wait()
        coupling_load.wait()

        def second_loop(v, carry):
            forward(v, False)

            @pl.when(me_w == top)
            def _():
                send_down(v, w)
                finish(v, w)

            return carry

        lax.fori_loop(0, VARS, second_loop, 0)

    for d in range(1, planes):
        plane_copy(d).wait()
    total = plane_sums[0]
    for i in range(1, planes):
        total = total + plane_sums[i]
    wall_own[...] = total
    wall_sums[me_w] = total
    for d in range(1, walls):
        wall_copy(d).start()

    @pl.when(me_w < top)
    def _():
        def third_loop(v, carry):
            bwd_copy(v).wait_recv()

            def emit(first, rows):
                x[v, pl.ds(first, SUB), :] = active * (w[v, pl.ds(first, SUB), :] - rows)

            apply_block(pv, lambda start: above[v, pl.ds(start, SUB), :], emit)

            @pl.when(me_w > 0)
            def _():
                send_down(v, x)

            finish(v, x)
            return carry

        lax.fori_loop(0, VARS, third_loop, 0)

    for d in range(1, walls):
        wall_copy(d).wait()
    total = wall_sums[0]
    for i in range(1, walls):
        total = total + wall_sums[i]
    mean[0, 0] = jnp.sum(total) / float(VARS * DOFS * 128 * planes * walls)

    def drain(v, carry):
        out_copy(v).wait()
        for side in range(2):
            for f in range(2):
                halo_copy(v, side, f).wait_send()

        @pl.when(me_w < top)
        def _():
            fwd_copy(v).wait_send()

        @pl.when(me_w > 0)
        def _():
            bwd_copy(v).wait_send()

        return carry

    lax.fori_loop(0, VARS, drain, 0)


def body(planes, walls, state, rhs, pivot_inv, coupling, face_coupling, neighbors, counts):
    lines = state.shape[3]
    assert state.shape[2] == 1 and lines == 128 and walls > 1
    rows = DOFS + 3
    face_rows = FACE + 7
    vectors = pltpu.VMEM((VARS, rows, lines), F32)
    dma = pltpu.SemaphoreType.DMA
    anywhere = pl.BlockSpec(memory_space=pl.ANY)
    new_state, mean = pl.pallas_call(
        functools.partial(kernel, planes, walls),
        out_shape=(
            jax.ShapeDtypeStruct(state.shape, F32),
            jax.ShapeDtypeStruct((1, 1), F32),
        ),
        in_specs=[anywhere] * 7,
        out_specs=(anywhere, pl.BlockSpec(memory_space=pltpu.SMEM)),
        scratch_shapes=[
            vectors,
            vectors,
            pltpu.VMEM((DOFS * DOFS, lines), F32),
            pltpu.VMEM((DOFS * DOFS, lines), F32),
            pltpu.VMEM((4 * FACE * FACE, lines), F32),
            pltpu.VMEM((4, lines), jnp.int32),
            pltpu.VMEM((1, lines), jnp.int32),
            pltpu.VMEM((VARS, 2, 2, face_rows, lines), F32),
            pltpu.VMEM((4, face_rows, lines), F32),
            vectors,
            pltpu.VMEM((rows, lines), F32),
            vectors,
            vectors,
            vectors,
            vectors,
            vectors,
            pltpu.VMEM((SUB, lines), F32),
            pltpu.VMEM((planes, SUB, lines), F32),
            pltpu.VMEM((SUB, lines), F32),
            pltpu.VMEM((walls, SUB, lines), F32),
            dma((7,)),
            dma((VARS,)),
            dma((VARS, 2, 2)),
            dma((VARS, 2, 2)),
            dma((VARS,)),
            dma((VARS,)),
            dma((VARS,)),
            dma((VARS,)),
            dma((planes,)),
            dma((planes,)),
            dma((walls,)),
            dma((walls,)),
        ],
        compiler_params=pltpu.CompilerParams(
            collective_id=0, has_side_effects=True, vmem_limit_bytes=40 * 2**20
        ),
        name="line_sweep",
    )(
        state, rhs, pivot_inv, coupling, face_coupling, neighbors.T, counts.reshape(1, lines)
    )
    return new_state, mean.reshape(())


def solution(mesh):
    planes, walls = mesh.shape["plane"], mesh.shape["wall"]
    field = P(None, None, "wall", "plane")
    return jax.shard_map(
        functools.partial(body, planes, walls),
        mesh=mesh,
        in_specs=(
            field, field, field, field,
            P(None, None, None, "wall", "plane"),
            P("plane", None),
            P("plane"),
        ),
        out_specs=(field, P()),
        check_vma=False,
    )
```

time: 404 us -> 50.8 us (0.13); the launches traced: 399 us -> 50.5 us
  matrix products: 219 us -> 0 us
  local copies, waits for them, and re-layouts: 67.4 us -> 8.57 us
  blocking collectives: 43.7 us -> 0 us
  Pallas kernels: 0 us -> 39.5 us
  waiting for transfers between devices: 32.7 us -> 0 us
  starting transfers between devices: 29.2 us -> 0 us
  other arithmetic: 4.34 us -> 0 us
    dot_general x19 -> x0, matrix products: 219 us -> none  [the longest x12 177 us: apply_block(): return jnp.einsum('jkl,vkl->vjl', block, vector, precision=highest)]
    psum x1 -> x0, blocking collectives: 43.7 us -> none  [body(): total = lax.psum(jnp.sum(residual * residual), ('plane', 'wall'))]
    pallas_call x0 -> x1, Pallas kernels: none -> 39.5 us  [body(): pl.pallas_call(functools.partial(kernel, planes, walls), out_shape=(jax.S...]
    ppermute x8 -> x0, waiting for transfers between devices: 32.7 us -> none  [the longest x6 32.7 us: from_behind(): lax.ppermute(value, axis, [(source, source + steps) for source in range(i...]
    ppermute x8 -> x0, starting transfers between devices: 29.2 us -> none  [the longest x6 23.1 us: from_behind(): lax.ppermute(value, axis, [(source, source + steps) for source in range(i...]
    while x14 -> x0, local copies, waits for them, and re-layouts: 26.6 us -> none  [the longest x2 26.6 us: body(): below = lax.fori_loop(0, wall_size - 1, forward_relay, zero_vector)]
    gather x4 -> x0, local copies, waits for them, and re-layouts: 11.5 us -> none  [body(): jnp.take(extended[opposite[face]], location[:, face], axis=3)]
    unnamed x31 -> x13, local copies, waits for them, and re-layouts: 18.9 us -> 8.57 us
  transfers between devices with their start and end apart: 8 -> 0, of which waited for: 6 -> 0; matrix products, arithmetic and copies ran while one was open for 10% -> 0% of each run, Pallas kernels for 0% -> 0%
where the time goes in v1:
time: 50.8 us; the launch traced here: 50.5 us
  Pallas kernels  39.5 us (78%)
  local copies, waits for them, and re-layouts  8.57 us (17%)
  between operations  2.47 us (5%)
    pallas_call x1, Pallas kernels, body(): pl.pallas_call(functools.partial(kernel, planes, walls), out_shape=(jax.S...  39.5 us
    unnamed x13, local copies, waits for them, and re-layouts  8.57 us

profile of v1, /device:TPU:0, one launch (start us, length us, event | category | flops | bytes accessed | tf_op | source)
XLA Modules:
  0.0 50.5 jit_solution(6876299768509373096)
XLA Ops:
  0.6 0.0 copy-start
  0.6 3.3 %copy-done = f32[125,125,1,128]{3,2,1,0:T(1,128)S(1)} copy-done((f32[125,125,1,128]{3,2,1,0:T(1,128)S(1)}, f32[125,125,1,128]{3,2,1,0:T(1,128)}, u32[]{:S(2)}) %copy-start) | copy-done | bytes 8000024
  3.9 0.0 copy-start.1
  3.9 1.3 %copy-done.1 = f32[4,25,25,1,128]{4,3,2,1,0:T(1,128)S(1)} copy-done((f32[4,25,25,1,128]{4,3,2,1,0:T(1,128)S(1)}, f32[4,25,25,1,128]{4,3,2,1,0:T(1,128)}, u32[]{:S(2)}) %copy-start.1) | copy-done | bytes 1280024
  5.2 0.0 copy-start.2
  5.2 1.0 %copy-done.2 = f32[5,125,1,128]{3,2,1,0:T(1,128)S(1)} copy-done((f32[5,125,1,128]{3,2,1,0:T(1,128)S(1)}, f32[5,125,1,128]{3,2,1,0:T(1,128)}, u32[]{:S(2)}) %copy-start.2) | copy-done | bytes 320024
  6.2 0.0 copy-start.3
  6.2 1.0 %copy-done.3 = f32[5,125,1,128]{3,2,1,0:T(1,128)S(1)} copy-done((f32[5,125,1,128]{3,2,1,0:T(1,128)S(1)}, f32[5,125,1,128]{3,2,1,0:T(1,128)}, u32[]{:S(2)}) %copy-start.3) | copy-done | bytes 320024
  7.2 0.0 copy-start.4
  7.2 0.7 %copy-done.4 = s32[128,4]{0,1:T(4,128)S(1)} copy-done((s32[128,4]{0,1:T(4,128)S(1)}, s32[128,4]{0,1:T(4,128)}, u32[]{:S(2)}) %copy-start.4) | copy-done | bytes 2072
  7.8 0.0 copy-start.5
  7.8 0.7 %copy-done.5 = s32[128]{0:T(128)S(1)} copy-done((s32[128]{0:T(128)S(1)}, s32[128]{0:T(128)}, u32[]{:S(2)}) %copy-start.5) | copy-done | bytes 536
  8.5 39.5 %line_sweep.1 = (f32[5,125,1,128]{3,2,1,0:T(1,128)S(1)}, f32[1,1]{1,0:T(1,128)}) custom-call(f32[5,125,1,128]{3,2,1,0:T(1,128)S(1)} %copy-done.2, f32[5,125,1,128]{3,2,1,0:T(1,128)S(1)} %copy-done.3, f32[125,125,1,128]{3,2,1,0:T(1,128)S(1)} %copy-done, f32[125,125,1,128]{3,2,1,0:T(1,128)} %coupling.1, f32[4,25,25,1,128]{4,3,2,1,0:T(1,128)S(1)} %copy-done.1, ...), custom_call_target="tpu_custom_call" | custom-call | tf_op jit(solution)/shard_map/line_sweep/pallas_call | solution.py:371
  48.0 0.7 %copy.11 = f32[5,125,1,128]{3,2,1,0:T(1,128)} copy(f32[5,125,1,128]{3,2,1,0:T(1,128)S(1)} %get-tuple-element.8) | data formatting | bytes 640000
Async XLA Ops:
  0.6 3.3 %copy-start = (f32[125,125,1,128]{3,2,1,0:T(1,128)S(1)}, f32[125,125,1,128]{3,2,1,0:T(1,128)}, u32[]{:S(2)}) copy-start(f32[125,125,1,128]{3,2,1,0:T(1,128)} %pivot.1) | copy-start | bytes 24000004
  3.9 1.3 %copy-start.1 = (f32[4,25,25,1,128]{4,3,2,1,0:T(1,128)S(1)}, f32[4,25,25,1,128]{4,3,2,1,0:T(1,128)}, u32[]{:S(2)}) copy-start(f32[4,25,25,1,128]{4,3,2,1,0:T(1,128)} %face.1) | copy-start | bytes 3840004
  5.2 1.0 %copy-start.2 = (f32[5,125,1,128]{3,2,1,0:T(1,128)S(1)}, f32[5,125,1,128]{3,2,1,0:T(1,128)}, u32[]{:S(2)}) copy-start(f32[5,125,1,128]{3,2,1,0:T(1,128)} %state.1) | copy-start | bytes 960004
  6.2 1.0 %copy-start.3 = (f32[5,125,1,128]{3,2,1,0:T(1,128)S(1)}, f32[5,125,1,128]{3,2,1,0:T(1,128)}, u32[]{:S(2)}) copy-start(f32[5,125,1,128]{3,2,1,0:T(1,128)} %rhs.1) | copy-start | bytes 960004
  7.2 0.7 %copy-start.4 = (s32[128,4]{0,1:T(4,128)S(1)}, s32[128,4]{0,1:T(4,128)}, u32[]{:S(2)}) copy-start(s32[128,4]{0,1:T(4,128)} %param.12) | copy-start | bytes 6148
  7.8 0.7 %copy-start.5 = (s32[128]{0:T(128)S(1)}, s32[128]{0:T(128)}, u32[]{:S(2)}) copy-start(s32[128]{0:T(128)} %param.13) | copy-start | bytes 1540

commit v2 on v1

--- a/solution.py
+++ b/solution.py
@@ -74,7 +74,7 @@
         )
 
     zeros = tuple(jnp.zeros((SUB, 128), F32) for _ in range(GROUPS))
-    totals = lax.fori_loop(0, DOFS, step, zeros, unroll=5)
+    totals = lax.fori_loop(0, DOFS, step, zeros, unroll=25)
     for t in range(GROUPS):
         store(STARTS[t], totals[t])
 
@@ -367,7 +367,7 @@
     face_rows = FACE + 7
     vectors = pltpu.VMEM((VARS, rows, lines), F32)
     dma = pltpu.SemaphoreType.DMA
-    anywhere = pl.BlockSpec(memory_space=pl.ANY)
+    anywhere = pl.BlockSpec(memory_space=pltpu.HBM)
     new_state, mean = pl.pallas_call(
         functools.partial(kernel, planes, walls),
         out_shape=(
@@ -411,7 +411,7 @@
             dma((walls,)),
         ],
         compiler_params=pltpu.CompilerParams(
-            collective_id=0, has_side_effects=True, vmem_limit_bytes=40 * 2**20
+            collective_id=0, has_side_effects=True, vmem_limit_bytes=67_043_328
         ),
         name="line_sweep",
     )(

time: 50.8 us -> 42.8 us (0.84)
  local copies, waits for them, and re-layouts: 8.57 us -> 1.72 us
  Pallas kernels: 39.5 us -> 38.5 us
    unnamed x13 -> x1, local copies, waits for them, and re-layouts: 8.57 us -> 1.72 us
    pallas_call x1, Pallas kernels: 39.5 us -> 38.5 us  [body(): pl.pallas_call(functools.partial(kernel, planes, walls), out_shape=(jax.S...]
where the time goes in v2:
time: 42.8 us; the launch traced here: 42.6 us
  Pallas kernels  38.5 us (90%)
  between operations  2.33 us (5%)
  local copies, waits for them, and re-layouts  1.72 us (4%)
    pallas_call x1, Pallas kernels, body(): pl.pallas_call(functools.partial(kernel, planes, walls), out_shape=(jax.S...  38.5 us
    unnamed x1, local copies, waits for them, and re-layouts  1.72 us

profile of v2, /device:TPU:0, one launch (start us, length us, event | category | flops | bytes accessed | tf_op | source)
XLA Modules:
  0.0 42.6 jit_solution(11412287025864159921)
XLA Ops:
  0.6 38.5 %line_sweep.1 = (f32[5,125,1,128]{3,2,1,0:T(1,128)}, f32[1,1]{1,0:T(1,128)}) custom-call(f32[5,125,1,128]{3,2,1,0:T(1,128)} %state.1, f32[5,125,1,128]{3,2,1,0:T(1,128)} %rhs.1, f32[125,125,1,128]{3,2,1,0:T(1,128)} %pivot.1, f32[125,125,1,128]{3,2,1,0:T(1,128)} %coupling.1, f32[4,25,25,1,128]{4,3,2,1,0:T(1,128)} %face.1, s32[4,128]{1,0:T(4,128)} %bitcast.3, ...), custom_call_target="tpu_custom_call" | custom-call | tf_op jit(solution)/shard_map/line_sweep/pallas_call | solution.py:371
  39.2 1.7 %copy.11 = f32[5,125,1,128]{3,2,1,0:T(1,128)} copy(f32[5,125,1,128]{3,2,1,0:T(1,128)} %get-tuple-element.8) | data formatting | bytes 640000

commit v3 on v2

--- a/solution.py
+++ b/solution.py
@@ -18,6 +18,7 @@
 
 STARTS = tuple(min(SUB * t, TAIL) for t in range(GROUPS))
 FACE_STARTS = tuple(min(SUB * t, FACE - SUB) for t in range(-(-FACE // SUB)))
+HALVES = (slice(0, SUB * (GROUPS // 2)), slice(SUB * (GROUPS // 2), DOFS))
 FACE_ROWS = ((DOFS - FACE, 1), (0, 1), (POINTS - 1, POINTS), (0, POINTS))
 
 
@@ -47,7 +48,7 @@
     return tiles
 
 
-def apply_block(block, load, emit):
+def apply_block(block, load, emit, halfway=None):
     tiles = vector_tiles(load)
 
     def group(g, carry):
@@ -62,21 +63,26 @@
         emit(first, row_sums(parts))
         return carry
 
-    lax.fori_loop(0, GROUPS, group, 0, unroll=2)
-
-
-def apply_transposed(block, load_row, store):
+    if halfway is None:
+        lax.fori_loop(0, GROUPS, group, 0, unroll=4)
+    else:
+        lax.fori_loop(0, GROUPS // 2, group, 0, unroll=4)
+        halfway()
+        lax.fori_loop(GROUPS // 2, GROUPS, group, 0, unroll=4)
+
+
+def apply_transposed(block, load_row, store, starts):
     def step(j, totals):
         spread = jnp.broadcast_to(load_row(j), (SUB, 128))
         return tuple(
-            totals[t] + block[pl.ds(j * DOFS + STARTS[t], SUB), :] * spread
-            for t in range(GROUPS)
-        )
-
-    zeros = tuple(jnp.zeros((SUB, 128), F32) for _ in range(GROUPS))
+            total + block[pl.ds(j * DOFS + start, SUB), :] * spread
+            for total, start in zip(totals, starts)
+        )
+
+    zeros = tuple(jnp.zeros((SUB, 128), F32) for _ in starts)
     totals = lax.fori_loop(0, DOFS, step, zeros, unroll=25)
-    for t in range(GROUPS):
-        store(STARTS[t], totals[t])
+    for start, total in zip(starts, totals):
+        store(start, total)
 
 
 def kernel(
@@ -116,11 +122,12 @@
         coupling_load.start()
 
     pl.semaphore_wait(barrier, planes - 1 + walls - 1)
+    loads[0].wait()
 
     def halo_copy(v, side, f):
         target = lax.rem(me_p + (1 if side == 0 else planes - 1), planes)
         return pltpu.make_async_remote_copy(
-            src_ref=state.at[v, pl.ds(FACE_ROWS[f][0], FACE), 0, :],
+            src_ref=st.at[v, pl.ds(FACE_ROWS[f][0], FACE), :],
             dst_ref=halo.at[v, side, f, 0:FACE, :],
             send_sem=halo_send.at[v, side, f],
             recv_sem=halo_recv.at[v, side, f],
@@ -135,21 +142,23 @@
 
     lax.fori_loop(0, VARS, send_halo, 0)
 
-    def fwd_copy(v):
+    def fwd_copy(v, half):
+        rows = HALVES[half]
         return pltpu.make_async_remote_copy(
-            src_ref=w.at[v, 0:DOFS, :],
-            dst_ref=below.at[v, 0:DOFS, :],
-            send_sem=fwd_send.at[v],
-            recv_sem=fwd_recv.at[v],
+            src_ref=w.at[v, rows, :],
+            dst_ref=below.at[v, rows, :],
+            send_sem=fwd_send.at[v, half],
+            recv_sem=fwd_recv.at[v, half],
             device_id={"wall": lax.rem(me_w + 1, walls)},
         )
 
-    def bwd_copy(v):
+    def bwd_copy(v, half):
+        rows = HALVES[half]
         return pltpu.make_async_remote_copy(
-            src_ref=back.at[v, 0:DOFS, :],
-            dst_ref=above.at[v, 0:DOFS, :],
-            send_sem=bwd_send.at[v],
-            recv_sem=bwd_recv.at[v],
+            src_ref=back.at[v, rows, :],
+            dst_ref=above.at[v, rows, :],
+            send_sem=bwd_send.at[v, half],
+            recv_sem=bwd_recv.at[v, half],
             device_id={"wall": lax.rem(me_w + walls - 1, walls)},
         )
 
@@ -175,7 +184,7 @@
         )
 
     ssq[...] = jnp.zeros((SUB, 128), F32)
-    for load in loads:
+    for load in loads[1:]:
         load.wait()
     active = jnp.broadcast_to(jnp.where(ct[...] > me_w, 1.0, 0.0).astype(F32), (SUB, 128))
     lane_bits = (st.shape[2] - 1).bit_length()
@@ -239,7 +248,8 @@
         if wall_element:
             source = lambda start: r[v, pl.ds(start, SUB), :]
         else:
-            fwd_copy(v).wait_recv()
+            for half in range(2):
+                fwd_copy(v, half).wait_recv()
 
             def emit_inner(first, rows):
                 inner[pl.ds(first, SUB), :] = r[v, pl.ds(first, SUB), :] - rows
@@ -250,18 +260,21 @@
         def emit(first, rows):
             w[v, pl.ds(first, SUB), :] = active * rows
 
-        apply_block(pv, source, emit)
-
-        @pl.when(me_w < top)
-        def _():
-            fwd_copy(v).start()
+        def send(half):
+            @pl.when(me_w < top)
+            def _():
+                fwd_copy(v, half).start()
+
+        apply_block(pv, source, emit, lambda: send(0))
+        send(1)
 
     def send_down(v, source):
         def store(start, rows):
             back[v, pl.ds(start, SUB), :] = rows
 
-        apply_transposed(cp, lambda j: source[v, pl.ds(j, 1), :], store)
-        bwd_copy(v).start()
+        for half, starts in enumerate((STARTS[: GROUPS // 2], STARTS[GROUPS // 2 :])):
+            apply_transposed(cp, lambda j: source[v, pl.ds(j, 1), :], store, starts)
+            bwd_copy(v, half).start()
 
     def finish(v, source):
         for start in STARTS:
@@ -299,11 +312,15 @@
             @pl.when(me_w == top)
             def _():
                 send_down(v, w)
+
+            return carry
+
+        lax.fori_loop(0, VARS, second_loop, 0)
+
+        @pl.when(me_w == top)
+        def _():
+            for v in range(VARS):
                 finish(v, w)
-
-            return carry
-
-        lax.fori_loop(0, VARS, second_loop, 0)
 
     for d in range(1, planes):
         plane_copy(d).wait()
@@ -318,7 +335,8 @@
     @pl.when(me_w < top)
     def _():
         def third_loop(v, carry):
-            bwd_copy(v).wait_recv()
+            for half in range(2):
+                bwd_copy(v, half).wait_recv()
 
             def emit(first, rows):
                 x[v, pl.ds(first, SUB), :] = active * (w[v, pl.ds(first, SUB), :] - rows)
@@ -349,11 +367,13 @@
 
         @pl.when(me_w < top)
         def _():
-            fwd_copy(v).wait_send()
+            for half in range(2):
+                fwd_copy(v, half).wait_send()
 
         @pl.when(me_w > 0)
         def _():
-            bwd_copy(v).wait_send()
+            for half in range(2):
+                bwd_copy(v, half).wait_send()
 
         return carry
 
@@ -401,10 +421,10 @@
             dma((VARS,)),
             dma((VARS, 2, 2)),
             dma((VARS, 2, 2)),
-            dma((VARS,)),
-            dma((VARS,)),
-            dma((VARS,)),
-            dma((VARS,)),
+            dma((VARS, 2)),
+            dma((VARS, 2)),
+            dma((VARS, 2)),
+            dma((VARS, 2)),
             dma((planes,)),
             dma((planes,)),
             dma((walls,)),

time: 42.8 us -> 41.3 us (0.965)
  Pallas kernels: 38.5 us -> 37.1 us
    pallas_call x1, Pallas kernels: 38.5 us -> 37.1 us  [body(): pl.pallas_call(functools.partial(kernel, planes, walls), out_shape=(jax.S...]
where the time goes in v3:
time: 41.3 us; the launch traced here: 41.1 us
  Pallas kernels  37.1 us (90%)
  between operations  2.33 us (6%)
  local copies, waits for them, and re-layouts  1.72 us (4%)
    pallas_call x1, Pallas kernels, body(): pl.pallas_call(functools.partial(kernel, planes, walls), out_shape=(jax.S...  37.1 us
    unnamed x1, local copies, waits for them, and re-layouts  1.72 us

profile of v3, /device:TPU:0, one launch (start us, length us, event | category | flops | bytes accessed | tf_op | source)
XLA Modules:
  0.0 41.1 jit_solution(9860511982146331719)
XLA Ops:
  0.6 37.1 %line_sweep.1 = (f32[5,125,1,128]{3,2,1,0:T(1,128)}, f32[1,1]{1,0:T(1,128)}) custom-call(f32[5,125,1,128]{3,2,1,0:T(1,128)} %state.1, f32[5,125,1,128]{3,2,1,0:T(1,128)} %rhs.1, f32[125,125,1,128]{3,2,1,0:T(1,128)} %pivot.1, f32[125,125,1,128]{3,2,1,0:T(1,128)} %coupling.1, f32[4,25,25,1,128]{4,3,2,1,0:T(1,128)} %face.1, s32[4,128]{1,0:T(4,128)} %bitcast.3, ...), custom_call_target="tpu_custom_call" | custom-call | tf_op jit(solution)/shard_map/line_sweep/pallas_call | solution.py:391
  37.7 1.7 %copy.11 = f32[5,125,1,128]{3,2,1,0:T(1,128)} copy(f32[5,125,1,128]{3,2,1,0:T(1,128)} %get-tuple-element.8) | data formatting | bytes 640000
